TPU v7x, 256 devices: a whole 4x4x8 slice. The times are simulated.
256 devices in a mesh: section: 2 (over core), seq: 16 (over x, y), head: 8 (over z).
Axes of the slice: x: 4, y: 4, z: 8, core: 2. Of those that a mesh axis runs over, the one named last changes fastest.
Arguments:
- x_in: bfloat16 [2, 4096, 8192], P('section', 'seq', 'head'), may hold values from -6 to 6
- b_in: bfloat16 [2, 4096, 2048], P('section', 'seq', 'head'), may hold values from -6 to 6
- c_in: bfloat16 [2, 4096, 2048], P('section', 'seq', 'head'), may hold values from -6 to 6
- z_in: bfloat16 [2, 4096, 8192], P('section', 'seq', 'head'), may hold values from -6 to 6
- dt_raw: float32 [2, 128, 4096], P('section', 'head', 'seq'), may hold values from -5 to 5
- conv_x: float32 [2, 4, 8192], P('section', None, 'head'), may hold values from -3 to 3
- conv_b: float32 [2, 4, 2048], P('section', None, 'head'), may hold values from -3 to 3
- conv_c: float32 [2, 4, 2048], P('section', None, 'head'), may hold values from -3 to 3
- a_rate: float32 [2, 128], P('section', 'head'), may hold values from 0.0001 to 1
- dt_bias: float32 [2, 128], P('section', 'head'), may hold values from -3 to -0.5
- skip_d: float32 [2, 128], P('section', 'head'), may hold values from 0.5 to 2
- norm_gain: float32 [2, 8192], P('section', 'head'), may hold values from 0.25 to 1.75
- out_weight: bfloat16 [2, 8192, 8192], P('section', 'head', 'seq'), may hold values from -0.0625 to 0.0625
Outputs:
- mixed: bfloat16 [2, 4096, 8192], P('section', ('seq', 'head'))
All inputs are finite; a program needn't handle non-finite values.
Results may differ from a plain program's by a relative error of at most 0.007.
Values may be sent and summed in bfloat16 or wider, within the bound.
A program may use at most 128 MiB of HBM per device.

v0:
```python
import jax
import jax.numpy as jnp
from jax import lax
from jax.sharding import Mesh
from jax.sharding import PartitionSpec as P

N = 256
SEQ = ("seq_0", "seq_1")
SEQ_HEAD = ("seq_0", "seq_1", "head")
epsilon = 1e-05


def passed_along(block, axis, distance):
    devices = range(lax.axis_size(axis))
    route = [(i - distance, i) for i in devices if i - distance in devices]
    return lax.ppermute(block, axis, route)


def neutral_like(x, identity):
    return jax.tree.map(
        lambda part, zero: jnp.zeros_like(part) + jnp.asarray(zero, part.dtype), x, identity
    )


def entering(x, axes, combine, identity):
    before = start = neutral_like(x, identity)
    so_far = x
    for axis in reversed(axes):
        size, place = (lax.axis_size(axis), lax.axis_index(axis))
        pieces = jax.tree.map(lambda part: lax.all_gather(part, axis), so_far)
        inside, so_far = (start, start)
        for k in range(size):
            passed = k < place
            so_far = combine(so_far, jax.tree.map(lambda part: part[k], pieces))
            inside = jax.tree.map(lambda new, old: jnp.where(passed, new, old), so_far, inside)
        before = combine(inside, before)
    return before


def from_everyone(x, axis):
    size = lax.axis_size(axis)
    return lax.all_to_all(jnp.broadcast_to(x[None], (size, *x.shape)), axis, 0, 0, tiled=True)


def in_order(pieces, dim):
    pieces = jnp.moveaxis(pieces, 0, dim)
    shape = pieces.shape
    return pieces.reshape(*shape[:dim], shape[dim] * shape[dim + 1], *shape[dim + 2 :])


def collect(x, axis, dim):
    pieces = from_everyone(x, axis)
    return in_order(pieces, dim)


def passed_along_2(block, axis, distance):
    devices = range(lax.axis_size(axis))
    route = [((i - distance) % len(devices), i) for i in devices]
    return lax.ppermute(block, axis, route)


def conv_silu(padded, kernel, length):
    kernel_taps = kernel.shape[0]
    summed = jnp.zeros((length, padded.shape[1]), jnp.float32)
    for offset in range(kernel_taps):
        summed = summed + kernel[offset] * padded[offset : offset + length].astype(jnp.float32)
    return jax.nn.silu(summed).astype(jnp.bfloat16)


def carry_combine(earlier, latter):
    return (earlier[0] * latter[0], latter[0][:, :, None, None] * earlier[1] + latter[1])


def per_device(
    x_in,
    b_in,
    c_in,
    z_in,
    dt_raw,
    conv_x,
    conv_b,
    conv_c,
    a_rate,
    dt_bias,
    skip_d,
    norm_gain,
    out_weight,
):
    x_local = x_in[0]
    b_local = b_in[0]
    c_local = c_in[0]
    length = x_local.shape[0]
    kernel_taps = conv_x.shape[1]
    x_cols = x_local.shape[1]
    b_cols = b_local.shape[1]
    edge_rows = jnp.concatenate(
        [
            x_local[length - kernel_taps + 1 :],
            b_local[length - kernel_taps + 1 :],
            c_local[length - kernel_taps + 1 :],
        ],
        axis=1,
    )
    before = passed_along(edge_rows, SEQ, 1)
    x_conv = conv_silu(jnp.concatenate([before[:, :x_cols], x_local], axis=0), conv_x[0], length)
    b_conv = conv_silu(
        jnp.concatenate([before[:, x_cols : x_cols + b_cols], b_local], axis=0), conv_b[0], length
    )
    c_conv = conv_silu(
        jnp.concatenate([before[:, x_cols + b_cols :], c_local], axis=0), conv_c[0], length
    )
    head_count = dt_raw.shape[1]
    group_count = b_cols // N
    per_group = head_count // group_count
    head_dim = x_cols // head_count
    step_size = jax.nn.softplus(dt_raw[0] + dt_bias[0][:, None])
    log_decay = jnp.cumsum(-a_rate[0][:, None] * step_size, axis=1)
    x_groups = x_conv.reshape(length, group_count, per_group, head_dim)
    b_groups = b_conv.reshape(length, group_count, N)
    c_groups = c_conv.reshape(length, group_count, N)
    log_groups = log_decay.reshape(group_count, per_group, length)
    step_groups = step_size.reshape(group_count, per_group, length)
    scores = jnp.einsum("tgn,ugn->gtu", c_groups, b_groups, preferred_element_type=jnp.float32)
    causal = jnp.arange(length)[:, None] >= jnp.arange(length)[None, :]
    spread_log = log_groups[:, :, :, None] - log_groups[:, :, None, :]
    damping = jnp.where(causal, jnp.exp(jnp.minimum(spread_log, 0.0)), 0.0)
    weights = (damping * step_groups[:, :, None, :] * scores[:, None]).astype(jnp.bfloat16)
    inside = jnp.einsum("gjtu,ugjp->tgjp", weights, x_groups, preferred_element_type=jnp.float32)
    to_end = jnp.exp(log_groups[:, :, -1:] - log_groups) * step_groups
    x_weighted = (
        x_groups.astype(jnp.float32) * jnp.transpose(to_end, (2, 0, 1))[..., None]
    ).astype(jnp.bfloat16)
    block_sum = jnp.einsum(
        "ugjp,ugn->gjpn", x_weighted, b_groups, preferred_element_type=jnp.float32
    )
    block_decay = jnp.exp(log_groups[:, :, -1])
    identity = (jnp.ones_like(block_decay), jnp.zeros_like(block_sum))
    carried_decay, carried = entering((block_decay, block_sum), SEQ, carry_combine, identity)
    carried_b = carried.astype(jnp.bfloat16)
    outside = jnp.einsum("tgn,gjpn->tgjp", c_groups, carried_b, preferred_element_type=jnp.float32)
    outside = outside * jnp.transpose(jnp.exp(log_groups), (2, 0, 1))[..., None]
    skip_term = skip_d[0].reshape(group_count, per_group)
    out_ssm = inside + outside + skip_term[None, :, :, None] * x_groups.astype(jnp.float32)
    gate_act = jax.nn.silu(z_in[0].astype(jnp.float32)).reshape(
        length, group_count, per_group * head_dim
    )
    gated = out_ssm.reshape(length, group_count, per_group * head_dim) * gate_act
    inverse_rms = lax.rsqrt(jnp.mean(gated * gated, axis=2, keepdims=True) + epsilon)
    hidden = ((gated * inverse_rms).reshape(length, x_cols) * norm_gain[0]).astype(jnp.bfloat16)
    local_weight = out_weight[0]
    full_columns = lax.all_gather(local_weight, "head", axis=0, tiled=True)
    owned_rows = lax.all_to_all(hidden, "head", split_axis=0, concat_axis=1, tiled=True)
    column_block = jnp.dot(
        collect(owned_rows, SEQ, 0), full_columns, preferred_element_type=jnp.float32
    ).astype(jnp.bfloat16)
    mixed = lax.all_to_all(column_block, SEQ, split_axis=0, concat_axis=1, tiled=True)
    passed = passed_along_2(mixed, "section", 1)
    return passed[None]


def solution(mesh):
    finer = Mesh(
        mesh.devices.reshape(mesh.shape["section"], 4, 4, mesh.shape["head"]),
        ("section", "seq_0", "seq_1", "head"),
    )
    return jax.shard_map(
        per_device,
        mesh=finer,
        in_specs=(
            P("section", SEQ, "head"),
            P("section", SEQ, "head"),
            P("section", SEQ, "head"),
            P("section", SEQ, "head"),
            P("section", "head", SEQ),
            P("section", None, "head"),
            P("section", None, "head"),
            P("section", None, "head"),
            P("section", "head"),
            P("section", "head"),
            P("section", "head"),
            P("section", "head"),
            P("section", "head", SEQ),
        ),
        out_specs=P("section", SEQ_HEAD, None),
        check_vma=False,
    )
```

profile of v0, /device:TPU:1, one launch (start us, length us, event | category | flops | bytes accessed | tf_op | source)
XLA Modules:
  0.0 360.7 jit_solution(4623957862641445590)
XLA Ops:
  6.5 0.7 slice_bitcast_fusion.4
  8.2 4.0 %collective-permute-start = (bf16[3,1536]{0,1:T(8,128)(2,1)S(1)}, bf16[3,1536]{0,1:T(8,128)(2,1)S(1)}, u32[]{:S(2)}, u32[]{:S(2)}) collective-permute-start(bf16[3,1536]{0,1:T(8,128)(2,1)S(1)} %copy.48), channel_id=1, source_target_pairs={{0,8},{8,16},{16,24},{24,32},{32,40},{40,48},{48,56},{56,64},{64,7... | collective-permute-start | bytes 27656 | tf_op jit(solution)/shard_map/ppermute | solution.py:16
  12.3 0.7 squeeze.21
  13.7 0.7 fusion.52
  15.5 0.8 exponential_bitcast_fusion
  16.3 0.9 fusion.59
  17.2 0.8 fusion.60
  18.0 1.2 copy.49
  19.3 0.8 collective-permute-done
  20.2 1.4 multiply_convert_fusion.6
  21.5 1.5 fusion.24
  23.0 1.3 fusion.50
  24.4 9.0 %all-gather = f32[4,16,1]{1,2,0:T(1,128)S(1)} all-gather(f32[1,16,1]{1,2,0:T(1,128)S(1)} %exp.90), channel_id=2, replica_groups=mesh['section'=2,'seq_0'=4,'seq_1'=4,'head'=8] {'seq_1'}, dimensions={0}, use_global_device_ids=true | all-gather | bytes 320 | tf_op jit(solution)/shard_map/all_gather | solution.py:30
  33.4 46.4 %all-gather.9.cloned.1.call-done = f32[64,64,256]{2,1,0:T(8,128)} async-done(((f32[16,64,256]{2,1,0:T(8,128)}), f32[64,64,256]{2,1,0:T(8,128)}) %all-gather.9.cloned.1.call-update) | async-done | bytes 4194320 | tf_op jit(solution)/shard_map/all_gather | solution.py:30
  79.8 3.6 %fusion.20 = f32[1,1,16,64,256]{4,3,2,1,0:T(8,128)} fusion(f32[64,64,256]{2,1,0:T(8,128)} %all-gather.9.cloned.1.call-done, f32[16]{0:T(128)S(1)} %get-tuple-element.31, f32[16]{0:T(128)S(1)} %get-tuple-element.30, f32[16]{0:T(128)S(1)} %get-tuple-element.24, f32[16]{0:T(128)S(1)} %get-tuple-element.32), kind=kLoop, calls=%fused_computation.25 | loop fusion | flops 1835008 | bytes 5243136 | tf_op jit(solution)/shard_map/add | solution.py:71
  84.5 1.1 convert_element_type.148
  85.6 7.6 %all_gather.22 = f32[4,1,16]{2,1,0:T(1,128)S(1)} all-gather(f32[1,1,16]{2,1,0:T(1,128)S(1)} %get-tuple-element.29), channel_id=1, replica_groups=mesh['section'=2,'seq_0'=4,'seq_1'=4,'head'=8] {'seq_0'}, dimensions={0}, use_global_device_ids=true | all-gather | bytes 320 | tf_op jit(solution)/shard_map/all_gather | solution.py:30
  94.0 2.5 fusion.9
  96.5 38.2 %all-gather.7.cloned.1.call-done = f32[4,1,16,64,256]{4,3,2,1,0:T(8,128)} async-done(((f32[1,1,16,64,256]{4,3,2,1,0:T(8,128)}), f32[4,1,16,64,256]{4,3,2,1,0:T(8,128)}) %all-gather.7.cloned.1.call-update) | async-done | bytes 4194320 | tf_op jit(solution)/shard_map/all_gather | solution.py:30
  134.7 5.7 %multiply_reduce_fusion = (f32[256]{0:T(256)S(1)}, f32[256,1,16,64]{0,3,2,1:T(8,128)}) fusion(f32[256,1,16,64]{0,3,2,1:T(8,128)S(1)} %bitcast.184, f32[16]{0:T(128)S(1)} %bitcast.209, f32[256,1,16,64]{0,3,2,1:T(8,128)} %fusion.9, f32[256,16]{0,1:T(8,128)S(1)} %get-tuple-element.9, bf16[256,256]{1,0:T(8,128)(2,1)S(1)} %multiply_convert_fusion.7, ...), kind=kOutput, calls=%fused_computation.35 | convolution fusion | flops 143392512 | bytes 12207688 | tf_op jit(solution)/shard_map/tgn,gjpn->tgjp/dot_general | solution.py:140
  140.4 2.5 copy.56
  143.6 1.6 multiply_convert_fusion.4
  145.2 29.7 %all_to_all.37 = bf16[8,32,1024]{2,1,0:T(8,128)(2,1)S(1)} all-to-all(bf16[8,32,1024]{2,1,0:T(8,128)(2,1)S(1)} %multiply_convert_fusion.4), channel_id=1, replica_groups=mesh['section'=2,'seq_0'=4,'seq_1'=4,'head'=8] {'head'}, dimensions={0} | all-to-all | bytes 1048576 | tf_op jit(solution)/shard_map/all_to_all | solution.py:152
  174.9 4.2 %broadcast_in_dim.36 = bf16[16,32,8192]{2,1,0:T(8,128)(2,1)} broadcast(bf16[32,8192]{1,0:T(8,128)(2,1)S(1)} %bitcast.181), dimensions={1,2} | broadcast | bytes 8912896 | tf_op jit(solution)/shard_map/broadcast_in_dim | solution.py:42
  179.2 5.7 %all-to-all-start.1 = ((bf16[16,32,8192]{2,1,0:T(8,128)(2,1)}), bf16[16,32,8192]{2,1,0:T(8,128)(2,1)}, u32[]{:S(2)}, u32[]{:S(2)}) async-start(bf16[16,32,8192]{2,1,0:T(8,128)(2,1)} %broadcast_in_dim.36), calls=%async_computation.1 | async-start | bytes 16777216 | tf_op jit(solution)/shard_map/all_to_all | solution.py:42
  184.8 57.4 %all-gather.11.cloned.1.call-done = bf16[1,8192,512]{2,1,0:T(8,128)(2,1)} async-done(((bf16[1,1024,512]{2,1,0:T(8,128)(2,1)}), bf16[1,8192,512]{2,1,0:T(8,128)(2,1)}) %all-gather.11.cloned.1.call-update) | async-done | bytes 8388624 | tf_op jit(solution)/shard_map/all_gather | solution.py:151
  242.2 74.1 %all-to-all-done.1 = bf16[16,32,8192]{2,1,0:T(8,128)(2,1)} async-done(((bf16[16,32,8192]{2,1,0:T(8,128)(2,1)}), bf16[16,32,8192]{2,1,0:T(8,128)(2,1)}, u32[]{:S(2)}, u32[]{:S(2)}) %all-to-all-start.1) | async-done | bytes 8388640 | tf_op jit(solution)/shard_map/all_to_all | solution.py:42
  316.4 10.2 %fusion.13 = bf16[512,512]{1,0:T(8,128)(2,1)S(1)} fusion(bf16[512,8192]{1,0:T(8,128)(2,1)} %bitcast.55, bf16[1,8192,512]{2,1,0:T(8,128)(2,1)} %all-gather.11.cloned.1.call-done), kind=kOutput, calls=%fused_computation.15 | convolution fusion | flops 4295229440 | bytes 17301504 | tf_op jit(solution)/shard_map/dot_general | solution.py:153
  326.6 19.9 %all_to_all.38 = bf16[16,32,512]{2,1,0:T(8,128)(2,1)S(1)} all-to-all(bf16[16,32,512]{2,1,0:T(8,128)(2,1)S(1)} %bitcast.189), channel_id=1, replica_groups=mesh['section'=2,'seq_0'=4,'seq_1'=4,'head'=8] {'seq_0','seq_1'}, dimensions={0} | all-to-all | bytes 1048576 | tf_op jit(solution)/shard_map/all_to_all | solution.py:156
  346.6 5.2 %collective-permute-start.1 = (bf16[32,8192]{1,0:T(8,128)(2,1)S(1)}, bf16[32,8192]{1,0:T(8,128)(2,1)S(1)}, u32[]{:S(2)}, u32[]{:S(2)}) collective-permute-start(bf16[32,8192]{1,0:T(8,128)(2,1)S(1)} %bitcast.187), channel_id=1, source_target_pairs={{128,0},{0,128},{129,1},{1,129},{130,2},{2,130},{131,3},{3,131},{1... | collective-permute-start | bytes 1572872 | tf_op jit(solution)/shard_map/ppermute | solution.py:59
  351.8 1.5 collective-permute-done.1
  353.3 0.8 copy.69
  (55 shorter events, 5.3 us)
Async XLA Ops:
  6.5 73.3 %all-gather.9.cloned.1.call-start = ((), (), s32[]{:S(2)}) async-start(), calls=%async_computation.4 | async-start | bytes 5242880 | tf_op jit(solution)/shard_map/all_gather | solution.py:30
  8.2 11.8 %collective-permute-start = (bf16[3,1536]{0,1:T(8,128)(2,1)S(1)}, bf16[3,1536]{0,1:T(8,128)(2,1)S(1)}, u32[]{:S(2)}, u32[]{:S(2)}) collective-permute-start(bf16[3,1536]{0,1:T(8,128)(2,1)S(1)} %copy.48), channel_id=1, source_target_pairs={{0,8},{8,16},{16,24},{24,32},{32,40},{40,48},{48,56},{56,64},{64,7... | collective-permute-start | bytes 27656 | tf_op jit(solution)/shard_map/ppermute | solution.py:16
  24.3 59.9 %copy-start.1 = (bf16[1,256,1024]{2,1,0:T(8,128)(2,1)S(1)}, bf16[1,256,1024]{2,1,0:T(8,128)(2,1)}, u32[]{:S(2)}) copy-start(bf16[1,256,1024]{2,1,0:T(8,128)(2,1)} %param.16) | copy-start | bytes 1572868
  24.3 110.4 %all-gather.7.cloned.1.call-start = ((), (), s32[]{:S(2)}) async-start(), calls=%async_computation.3 | async-start | bytes 5242880 | tf_op jit(solution)/shard_map/all_gather | solution.py:30
  79.8 13.4 %copy-start.6 = (f32[1,4,256]{2,1,0:T(4,128)S(1)}, f32[1,4,256]{2,1,0:T(4,128)}, u32[]{:S(2)}) copy-start(f32[1,4,256]{2,1,0:T(4,128)} %param.20) | copy-start | bytes 12292
  79.8 13.4 %copy-start.2 = (f32[1,16,256]{2,1,0:T(8,128)S(1)}, f32[1,16,256]{2,1,0:T(8,128)}, u32[]{:S(2)}) copy-start(f32[1,16,256]{2,1,0:T(8,128)} %param.17) | copy-start | bytes 49156
  79.8 13.4 %copy-start.4 = (f32[1,16]{1,0:T(1,128)S(1)}, f32[1,16]{1,0:T(1,128)}, u32[]{:S(2)}) copy-start(f32[1,16]{1,0:T(1,128)} %param.22) | copy-start | bytes 196
  79.8 13.7 %copy-start.3 = (bf16[1,256,256]{2,1,0:T(8,128)(2,1)S(1)}, bf16[1,256,256]{2,1,0:T(8,128)(2,1)}, u32[]{:S(2)}) copy-start(bf16[1,256,256]{2,1,0:T(8,128)(2,1)} %param.15) | copy-start | bytes 393220
  83.5 158.7 %all-gather.11.cloned.1.call-start = ((), (), s32[]{:S(2)}) async-start(), calls=%async_computation.5 | async-start | bytes 9437184 | tf_op jit(solution)/shard_map/all_gather | solution.py:151
  93.7 41.0 %copy-start = (f32[1,1,16,64,256]{4,3,2,1,0:T(8,128)S(1)}, f32[1,1,16,64,256]{4,3,2,1,0:T(8,128)}, u32[]{:S(2)}) copy-start(f32[1,1,16,64,256]{4,3,2,1,0:T(8,128)} %fusion.20) | copy-start | bytes 3145732
  93.7 41.0 %copy-start.7 = (f32[1,16]{1,0:T(1,128)S(1)}, f32[1,16]{1,0:T(1,128)}, u32[]{:S(2)}) copy-start(f32[1,16]{1,0:T(1,128)} %param.23) | copy-start | bytes 196
  140.4 3.2 copy-start.5
  179.2 137.2 %all-to-all-start.1 = ((bf16[16,32,8192]{2,1,0:T(8,128)(2,1)}), bf16[16,32,8192]{2,1,0:T(8,128)(2,1)}, u32[]{:S(2)}, u32[]{:S(2)}) async-start(bf16[16,32,8192]{2,1,0:T(8,128)(2,1)} %broadcast_in_dim.36), calls=%async_computation.1 | async-start | bytes 16777216 | tf_op jit(solution)/shard_map/all_to_all | solution.py:42
  346.6 6.7 %collective-permute-start.1 = (bf16[32,8192]{1,0:T(8,128)(2,1)S(1)}, bf16[32,8192]{1,0:T(8,128)(2,1)S(1)}, u32[]{:S(2)}, u32[]{:S(2)}) collective-permute-start(bf16[32,8192]{1,0:T(8,128)(2,1)S(1)} %bitcast.187), channel_id=1, source_target_pairs={{128,0},{0,128},{129,1},{1,129},{130,2},{2,130},{131,3},{3,131},{1... | collective-permute-start | bytes 1572872 | tf_op jit(solution)/shard_map/ppermute | solution.py:59
Sparse Core Ops, SparseCore 0:
  24.5 55.3 all-gather.8
  83.6 51.0 all-gather.6
  136.5 105.6 all-gather.10
where the time goes:
time: 361 us
  waiting for transfers between devices  219 us (61%)
  blocking collectives  66.2 us (18%)
  matrix products  19.9 us (6%)
  starting transfers between devices  15 us (4%)
  local copies, waits for them, and re-layouts  14.5 us (4%)
  between operations  13.4 us (4%)
  other arithmetic  12.5 us (3%)
    all_gather x2, waiting for transfers between devices, entering(): pieces = jax.tree.map(lambda part: lax.all_gather(part, axis), so_far)  84.7 us
    all_to_all x1, waiting for transfers between devices, from_everyone(): lax.all_to_all(jnp.broadcast_to(x[None], (size, *x.shape)), axis, 0, 0, t...  74.1 us
    all_gather x1, waiting for transfers between devices, per_device(): full_columns = lax.all_gather(local_weight, 'head', axis=0, tiled=True)  57.4 us
    all_to_all x1, blocking collectives, per_device(): lax.all_to_all(hidden, 'head', split_axis=0, concat_axis=1, tiled=True)  29.7 us
    all_to_all x1, blocking collectives, per_device(): lax.all_to_all(column_block, SEQ, split_axis=0, concat_axis=1, tiled=True)  19.9 us
    all_gather x2, blocking collectives, entering(): pieces = jax.tree.map(lambda part: lax.all_gather(part, axis), so_far)  16.6 us
    dot_general x1, matrix products, per_device(): jnp.dot(collect(owned_rows, SEQ, 0), full_columns, preferred_element_type...  10.2 us
  transfers between devices with their start and end apart: 6, of which 6 were waited for; matrix products, arithmetic and copies ran while one was open for 7% of the time, Pallas kernels for 0%

commit v1 on v0

--- a/solution.py
+++ b/solution.py
@@ -148,7 +148,9 @@
     inverse_rms = lax.rsqrt(jnp.mean(gated * gated, axis=2, keepdims=True) + epsilon)
     hidden = ((gated * inverse_rms).reshape(length, x_cols) * norm_gain[0]).astype(jnp.bfloat16)
     local_weight = out_weight[0]
-    full_columns = lax.all_gather(local_weight, "head", axis=0, tiled=True)
+    full_columns = jnp.concatenate(
+        lax.all_to_all(jnp.stack([local_weight] * lax.axis_size("head")), "head", 0, 0), axis=0
+    )
     owned_rows = lax.all_to_all(hidden, "head", split_axis=0, concat_axis=1, tiled=True)
     column_block = jnp.dot(
         collect(owned_rows, SEQ, 0), full_columns, preferred_element_type=jnp.float32

time: 361 us -> 499 us (1.38)
  blocking collectives: 66.2 us -> 153 us
  waiting for transfers between devices: 219 us -> 275 us
    all_to_all x1, waiting for transfers between devices: 74.1 us -> 187 us  [per_device(): lax.all_to_all(jnp.stack([local_weight] * lax.axis_size('head')), 'head',...]
    all_to_all x0 -> x1, blocking collectives: none -> 100 us  [from_everyone(): lax.all_to_all(jnp.broadcast_to(x[None], (size, *x.shape)), axis, 0, 0, t...]
    all_gather x1 -> x0, waiting for transfers between devices: 57.4 us -> none  [per_device(): full_columns = lax.all_gather(local_weight, 'head', axis=0, tiled=True)]
    all_to_all x1, blocking collectives: 29.7 us -> 22.4 us  [per_device(): lax.all_to_all(hidden, 'head', split_axis=0, concat_axis=1, tiled=True)]
    all_to_all x1, blocking collectives: 19.9 us -> 13.7 us  [per_device(): lax.all_to_all(column_block, SEQ, split_axis=0, concat_axis=1, tiled=True)]
  transfers between devices with their start and end apart: 6 -> 5, of which waited for: 6 -> 5; matrix products, arithmetic and copies ran while one was open for 7% -> 2% of each run, Pallas kernels for 0% -> 0%
where the time goes in v1:
time: 499 us; the launch traced here: 498 us
  waiting for transfers between devices  275 us (55%)
  blocking collectives  153 us (31%)
  matrix products  16.6 us (3%)
  local copies, waits for them, and re-layouts  15.2 us (3%)
  between operations  13.7 us (3%)
  other arithmetic  12.7 us (3%)
  starting transfers between devices  12.3 us (2%)
    all_to_all x1, waiting for transfers between devices, per_device(): lax.all_to_all(jnp.stack([local_weight] * lax.axis_size('head')), 'head',...  187 us
    all_to_all x1, blocking collectives, from_everyone(): lax.all_to_all(jnp.broadcast_to(x[None], (size, *x.shape)), axis, 0, 0, t...  100 us
    all_gather x2, waiting for transfers between devices, entering(): pieces = jax.tree.map(lambda part: lax.all_gather(part, axis), so_far)  85.4 us
    all_to_all x1, blocking collectives, per_device(): lax.all_to_all(hidden, 'head', split_axis=0, concat_axis=1, tiled=True)  22.4 us
    all_gather x2, blocking collectives, entering(): pieces = jax.tree.map(lambda part: lax.all_gather(part, axis), so_far)  16.5 us
    all_to_all x1, blocking collectives, per_device(): lax.all_to_all(column_block, SEQ, split_axis=0, concat_axis=1, tiled=True)  13.7 us
  transfers between devices with their start and end apart: 5, of which 5 were waited for; matrix products, arithmetic and copies ran while one was open for 2% of the time, Pallas kernels for 0%

profile of v1, /device:TPU:1, one launch (start us, length us, event | category | flops | bytes accessed | tf_op | source)
XLA Modules:
  0.0 498.0 jit_solution(9144693629647523797)
XLA Ops:
  8.2 4.0 collective-permute-start
  13.0 0.7 squeeze.19
  13.7 0.7 fusion.47
  15.5 0.9 fusion.54
  16.4 0.8 exponential_bitcast_fusion
  17.2 0.8 fusion.55
  18.1 1.2 copy.49
  19.3 0.8 collective-permute-done
  20.2 1.4 multiply_convert_fusion.6
  21.6 1.5 fusion.19
  23.1 1.3 fusion.45
  24.5 8.9 %all-gather = f32[4,16,1]{1,2,0:T(1,128)S(1)} all-gather(f32[1,16,1]{1,2,0:T(1,128)S(1)} %exp.90), channel_id=2, replica_groups=mesh['section'=2,'seq_0'=4,'seq_1'=4,'head'=8] {'seq_1'}, dimensions={0}, use_global_device_ids=true | all-gather | bytes 320 | tf_op jit(solution)/shard_map/all_gather | solution.py:30
  33.3 46.5 %all-gather.7.cloned.1.call-done = f32[64,64,256]{2,1,0:T(8,128)} async-done(((f32[16,64,256]{2,1,0:T(8,128)}), f32[64,64,256]{2,1,0:T(8,128)}) %all-gather.7.cloned.1.call-update) | async-done | bytes 4194320 | tf_op jit(solution)/shard_map/all_gather | solution.py:30
  79.9 3.6 fusion.15
  83.8 1.2 convert_element_type.148
  84.9 7.6 %all_gather.19 = f32[4,1,16]{2,1,0:T(1,128)S(1)} all-gather(f32[1,1,16]{2,1,0:T(1,128)S(1)} %get-tuple-element.29), channel_id=1, replica_groups=mesh['section'=2,'seq_0'=4,'seq_1'=4,'head'=8] {'seq_0'}, dimensions={0}, use_global_device_ids=true | all-gather | bytes 320 | tf_op jit(solution)/shard_map/all_gather | solution.py:30
  93.3 2.5 fusion.7
  95.9 38.9 %all-gather.5.cloned.1.call-done = f32[4,1,16,64,256]{4,3,2,1,0:T(8,128)} async-done(((f32[1,1,16,64,256]{4,3,2,1,0:T(8,128)}), f32[4,1,16,64,256]{4,3,2,1,0:T(8,128)}) %all-gather.5.cloned.1.call-update) | async-done | bytes 4194320 | tf_op jit(solution)/shard_map/all_gather | solution.py:30
  134.8 5.7 %multiply_reduce_fusion = (f32[256]{0:T(256)S(1)}, f32[256,1,16,64]{0,3,2,1:T(8,128)}) fusion(f32[256,1,16,64]{0,3,2,1:T(8,128)S(1)} %bitcast.184, f32[16]{0:T(128)S(1)} %bitcast.209, f32[256,1,16,64]{0,3,2,1:T(8,128)} %fusion.7, f32[256,16]{0,1:T(8,128)S(1)} %get-tuple-element.9, bf16[256,256]{1,0:T(8,128)(2,1)S(1)} %multiply_convert_fusion.7, ...), kind=kOutput, calls=%fused_computation.33 | convolution fusion | flops 143392512 | bytes 12207688 | tf_op jit(solution)/shard_map/tgn,gjpn->tgjp/dot_general | solution.py:140
  140.5 2.5 copy.56
  143.6 1.7 multiply_convert_fusion.4
  145.3 22.4 %all_to_all.42 = bf16[8,32,1024]{2,1,0:T(8,128)(2,1)S(1)} all-to-all(bf16[8,32,1024]{2,1,0:T(8,128)(2,1)S(1)} %multiply_convert_fusion.4), channel_id=1, replica_groups=mesh['section'=2,'seq_0'=4,'seq_1'=4,'head'=8] {'head'}, dimensions={0} | all-to-all | bytes 1048576 | tf_op jit(solution)/shard_map/all_to_all | solution.py:154
  167.7 4.0 stack.3
  171.7 5.0 all-to-all-start.2
  176.7 186.8 %all-to-all-done.2 = bf16[8,1024,512]{2,1,0:T(8,128)(2,1)} async-done(((bf16[8,1024,512]{2,1,0:T(8,128)(2,1)}), bf16[8,1024,512]{2,1,0:T(8,128)(2,1)}, u32[]{:S(2)}, u32[]{:S(2)}) %all-to-all-start.2) | async-done | bytes 8388640 | tf_op jit(solution)/shard_map/all_to_all | solution.py:152
  363.5 1.0 broadcast_in_dim.36
  364.5 100.4 %all_to_all.43 = bf16[16,32,8192]{2,1,0:T(8,128)(2,1)S(1)} all-to-all(bf16[16,32,8192]{2,1,0:T(8,128)(2,1)S(1)} %broadcast_in_dim.36), channel_id=1, replica_groups=mesh['section'=2,'seq_0'=4,'seq_1'=4,'head'=8] {'seq_0','seq_1'}, dimensions={0} | all-to-all | bytes 16777216 | tf_op jit(solution)/shard_map/all_to_all | solution.py:42
  464.9 6.9 %convolution_convert_fusion = bf16[512,512]{1,0:T(8,128)(2,1)S(1)} fusion(bf16[512,8192]{1,0:T(8,128)(2,1)S(1)} %bitcast.176, bf16[8192,512]{1,0:T(8,128)(2,1)} %bitcast.57), kind=kOutput, calls=%fused_computation.13 | convolution fusion | flops 4295229440 | bytes 17301504 | tf_op jit(solution)/shard_map/dot_general | solution.py:155
  471.8 13.7 %all_to_all.44 = bf16[16,32,512]{2,1,0:T(8,128)(2,1)S(1)} all-to-all(bf16[16,32,512]{2,1,0:T(8,128)(2,1)S(1)} %bitcast.189), channel_id=1, replica_groups=mesh['section'=2,'seq_0'=4,'seq_1'=4,'head'=8] {'seq_0','seq_1'}, dimensions={0} | all-to-all | bytes 1048576 | tf_op jit(solution)/shard_map/all_to_all | solution.py:158
  485.5 3.3 collective-permute-start.1
  488.8 1.5 collective-permute-done.1
  490.3 0.8 copy.69
  (56 shorter events, 5.3 us)
Async XLA Ops:
  6.5 73.3 %all-gather.7.cloned.1.call-start = ((), (), s32[]{:S(2)}) async-start(), calls=%async_computation.5 | async-start | bytes 5242880 | tf_op jit(solution)/shard_map/all_gather | solution.py:30
  8.2 11.8 %collective-permute-start = (bf16[3,1536]{0,1:T(8,128)(2,1)S(1)}, bf16[3,1536]{0,1:T(8,128)(2,1)S(1)}, u32[]{:S(2)}, u32[]{:S(2)}) collective-permute-start(bf16[3,1536]{0,1:T(8,128)(2,1)S(1)} %copy.48), channel_id=1, source_target_pairs={{0,8},{8,16},{16,24},{24,32},{32,40},{40,48},{48,56},{56,64},{64,7... | collective-permute-start | bytes 27656 | tf_op jit(solution)/shard_map/ppermute | solution.py:16
  23.1 60.5 %copy-start.1 = (bf16[1,256,1024]{2,1,0:T(8,128)(2,1)S(1)}, bf16[1,256,1024]{2,1,0:T(8,128)(2,1)}, u32[]{:S(2)}) copy-start(bf16[1,256,1024]{2,1,0:T(8,128)(2,1)} %param.16) | copy-start | bytes 1572868
  24.4 110.4 %all-gather.5.cloned.1.call-start = ((), (), s32[]{:S(2)}) async-start(), calls=%async_computation.4 | async-start | bytes 5242880 | tf_op jit(solution)/shard_map/all_gather | solution.py:30
  79.9 12.7 %copy-start.7 = (f32[1,4,256]{2,1,0:T(4,128)S(1)}, f32[1,4,256]{2,1,0:T(4,128)}, u32[]{:S(2)}) copy-start(f32[1,4,256]{2,1,0:T(4,128)} %param.20) | copy-start | bytes 12292
  79.9 12.7 %copy-start.3 = (f32[1,16,256]{2,1,0:T(8,128)S(1)}, f32[1,16,256]{2,1,0:T(8,128)}, u32[]{:S(2)}) copy-start(f32[1,16,256]{2,1,0:T(8,128)} %param.17) | copy-start | bytes 49156
  79.9 12.8 %copy-start.5 = (f32[1,16]{1,0:T(1,128)S(1)}, f32[1,16]{1,0:T(1,128)}, u32[]{:S(2)}) copy-start(f32[1,16]{1,0:T(1,128)} %param.22) | copy-start | bytes 196
  79.9 13.0 %copy-start.4 = (bf16[1,256,256]{2,1,0:T(8,128)(2,1)S(1)}, bf16[1,256,256]{2,1,0:T(8,128)(2,1)}, u32[]{:S(2)}) copy-start(bf16[1,256,256]{2,1,0:T(8,128)(2,1)} %param.15) | copy-start | bytes 393220
  93.1 41.7 %copy-start = (f32[1,1,16,64,256]{4,3,2,1,0:T(8,128)S(1)}, f32[1,1,16,64,256]{4,3,2,1,0:T(8,128)}, u32[]{:S(2)}) copy-start(f32[1,1,16,64,256]{4,3,2,1,0:T(8,128)} %fusion.15) | copy-start | bytes 3145732
  93.1 41.7 %copy-start.8 = (f32[1,16]{1,0:T(1,128)S(1)}, f32[1,16]{1,0:T(1,128)}, u32[]{:S(2)}) copy-start(f32[1,16]{1,0:T(1,128)} %param.23) | copy-start | bytes 196
  140.4 3.2 copy-start.6
  143.6 24.1 %copy-start.2 = (bf16[1,1024,512]{2,1,0:T(8,128)(2,1)S(1)}, bf16[1,1024,512]{2,1,0:T(8,128)(2,1)}, u32[]{:S(2)}) copy-start(bf16[1,1024,512]{2,1,0:T(8,128)(2,1)} %param.25) | copy-start | bytes 3145732
  171.7 191.8 %all-to-all-start.2 = ((bf16[8,1024,512]{2,1,0:T(8,128)(2,1)}), bf16[8,1024,512]{2,1,0:T(8,128)(2,1)}, u32[]{:S(2)}, u32[]{:S(2)}) async-start(bf16[8,1024,512]{2,1,0:T(8,128)(2,1)} %stack.3), calls=%async_computation.2 | async-start | bytes 16777216 | tf_op jit(solution)/shard_map/all_to_all | solution.py:152
  485.5 4.8 collective-permute-start.1
Sparse Core Ops, SparseCore 0:
  24.5 55.3 all-gather.6
  83.7 51.0 all-gather.4
